TPU v7x, 32 devices: a whole 2x2x4 slice. The times are simulated.
32 devices in a mesh: dp: 4 (over y, x), ctx: 8 (over z, core).
Axes of the slice: x: 2, y: 2, z: 4, core: 2. Of those that a mesh axis runs over, the one named last changes fastest.
Arguments:
- inputs: bfloat16 [4, 16, 128, 2048], P('dp', 'ctx'), may hold values from -6 to 6
- block_of: int32 [4, 16], P('dp', 'ctx'), may hold values from 0 to 15, as said below
- first_gain: float32 [2048], P('dp'), may hold values from 0.5 to 1.5
- first_shift: float32 [2048], P('dp'), may hold values from -3 to 3
- w_qkv: bfloat16 [2048, 6144], P('dp'), may hold values from -8 to 8
- qkv_bias: float32 [6144], P('dp'), may hold values from -3 to 3
- w_out: bfloat16 [2048, 2048], P('dp'), may hold values from -0.75 to 0.75
- second_gain: float32 [2048], P('dp'), may hold values from 0.5 to 1.5
- second_shift: float32 [2048], P('dp'), may hold values from -3 to 3
- w_gateup: bfloat16 [2048, 11264], P('dp'), may hold values from -0.125 to 0.125
- w_down: bfloat16 [5632, 2048], P('dp'), may hold values from -0.078125 to 0.078125
- cotangent: bfloat16 [4, 16, 128, 2048], P('dp', 'ctx'), may hold values from -6 to 6
Outputs:
- outputs: bfloat16 [4, 16, 128, 2048], P('dp', 'ctx')
- grad_inputs: float32 [4, 16, 128, 2048], P('dp', 'ctx')
- grad_first_gain: float32 [2048], P('dp')
- grad_first_shift: float32 [2048], P('dp')
- grad_w_qkv: float32 [2048, 6144], P('dp')
- grad_qkv_bias: float32 [6144], P('dp')
- grad_w_out: float32 [2048, 2048], P('dp')
- grad_second_gain: float32 [2048], P('dp')
- grad_second_shift: float32 [2048], P('dp')
- grad_w_gateup: float32 [2048, 11264], P('dp')
- grad_w_down: float32 [5632, 2048], P('dp')
Inputs may be any that keep to these rules, and one draw needn't show every extreme that they name: `block_of`: for each sequence the 16 entries are a permutation of the blocks, and the two slots of one index of ctx hold blocks b and 15 - b, in either order.
All inputs are finite; a program needn't handle non-finite values.
Results may differ from a plain program's by a relative error of at most 0.035.
Values may be sent and summed in bfloat16 or wider, within the bound.
A program may use at most 640 MiB of HBM per device.

v0:
```python
import jax
import jax.numpy as jnp
from jax import lax
from jax.sharding import PartitionSpec as P

HEADS = 32
HEAD_DIM = 64
ROT = 16
epsilon = 1e-05


def layer_norm(token_rows, gain_vec, shift_vec):
    centre = jnp.mean(token_rows, axis=-1, keepdims=True)
    centred = token_rows - centre
    spread = jnp.mean(centred * centred, axis=-1, keepdims=True)
    inverse = lax.rsqrt(spread + epsilon)
    normed = centred * inverse
    return (normed * gain_vec + shift_vec, normed, inverse)


def norm_back(grad_rows, normed, inverse, gain_vec):
    scaled = grad_rows * gain_vec
    mean_plain = jnp.mean(scaled, axis=-1, keepdims=True)
    mean_cross = jnp.mean(scaled * normed, axis=-1, keepdims=True)
    return inverse * (scaled - mean_plain - normed * mean_cross)


def rotary_tables(positions):
    half_rot = ROT // 2
    frequency = 10000.0 ** (-2.0 * jnp.arange(half_rot, dtype=jnp.float32) / ROT)
    angles = positions.astype(jnp.float32)[:, None] * frequency[None, :]
    return (jnp.cos(angles), jnp.sin(angles))


def rotate_heads(head_rows, cosine, sine_part, direction_sign):
    half_rot = ROT // 2
    first_half = head_rows[..., :half_rot]
    second_half = head_rows[..., half_rot:ROT]
    cos_rows = cosine[:, None, :]
    sin_rows = sine_part[:, None, :] * direction_sign
    return jnp.concatenate(
        [
            first_half * cos_rows - second_half * sin_rows,
            second_half * cos_rows + first_half * sin_rows,
            head_rows[..., ROT:],
        ],
        axis=-1,
    )


def attend(query, keys_all, values_all, query_pos, key_pos):
    tok_count, head_count, head_width = query.shape
    per_group = min(4, head_count)
    score_scale = head_width ** (-0.5)
    allowed = key_pos[None, :] <= query_pos[:, None]

    def group_step(group_index, carry):
        output_all, lse_all = carry
        first_head = jnp.asarray(group_index).astype(jnp.int32) * per_group
        query_part = lax.dynamic_slice_in_dim(query, first_head, per_group, 1)
        keys_part = lax.dynamic_slice_in_dim(keys_all, first_head, per_group, 1)
        values_part = lax.dynamic_slice_in_dim(values_all, first_head, per_group, 1)
        scores = (
            jnp.einsum("thd,shd->hts", query_part, keys_part, preferred_element_type=jnp.float32)
            * score_scale
        )
        scores = jnp.where(allowed[None], scores, -jnp.inf)
        row_max = jnp.max(scores, axis=-1, keepdims=True)
        log_total = row_max + jnp.log(jnp.sum(jnp.exp(scores - row_max), axis=-1, keepdims=True))
        weights = jnp.exp(scores - log_total).astype(jnp.bfloat16)
        mixed = jnp.einsum(
            "hts,shd->thd", weights, values_part, preferred_element_type=jnp.float32
        ).astype(jnp.bfloat16)
        output_all = lax.dynamic_update_slice_in_dim(output_all, mixed, first_head, 1)
        lse_all = lax.dynamic_update_slice_in_dim(lse_all, log_total[..., 0], first_head, 0)
        return (output_all, lse_all)

    init = (jnp.zeros(query.shape, jnp.bfloat16), jnp.zeros((head_count, tok_count), jnp.float32))
    return lax.fori_loop(0, head_count // per_group, group_step, init)


def attend_back(query, keys_all, values_all, output, grad_output, lse_all, query_pos, key_pos):
    tok_count, head_count, head_width = query.shape
    per_group = min(4, head_count)
    score_scale = head_width ** (-0.5)
    allowed = key_pos[None, :] <= query_pos[:, None]
    delta_all = jnp.einsum(
        "thd,thd->ht", output.astype(jnp.float32), grad_output.astype(jnp.float32)
    )

    def group_step(group_index, carry):
        grad_q_all, grad_k_all, grad_v_all = carry
        first_head = jnp.asarray(group_index).astype(jnp.int32) * per_group
        query_part = lax.dynamic_slice_in_dim(query, first_head, per_group, 1)
        keys_part = lax.dynamic_slice_in_dim(keys_all, first_head, per_group, 1)
        values_part = lax.dynamic_slice_in_dim(values_all, first_head, per_group, 1)
        dout_part = lax.dynamic_slice_in_dim(grad_output, first_head, per_group, 1)
        lse_part = lax.dynamic_slice_in_dim(lse_all, first_head, per_group, 0)
        delta_part = lax.dynamic_slice_in_dim(delta_all, first_head, per_group, 0)
        scores = (
            jnp.einsum("thd,shd->hts", query_part, keys_part, preferred_element_type=jnp.float32)
            * score_scale
        )
        scores = jnp.where(allowed[None], scores, -jnp.inf)
        probs = jnp.exp(scores - lse_part[..., None])
        probs_low = probs.astype(jnp.bfloat16)
        grad_v_part = jnp.einsum(
            "hts,thd->shd", probs_low, dout_part, preferred_element_type=jnp.float32
        )
        grad_p = jnp.einsum(
            "thd,shd->hts", dout_part, values_part, preferred_element_type=jnp.float32
        )
        grad_s = (probs * (grad_p - delta_part[..., None])).astype(jnp.bfloat16)
        grad_q_part = (
            jnp.einsum("hts,shd->thd", grad_s, keys_part, preferred_element_type=jnp.float32)
            * score_scale
        )
        grad_k_part = (
            jnp.einsum("hts,thd->shd", grad_s, query_part, preferred_element_type=jnp.float32)
            * score_scale
        )
        grad_q_all = lax.dynamic_update_slice_in_dim(grad_q_all, grad_q_part, first_head, 1)
        grad_k_all = lax.dynamic_update_slice_in_dim(grad_k_all, grad_k_part, first_head, 1)
        grad_v_all = lax.dynamic_update_slice_in_dim(grad_v_all, grad_v_part, first_head, 1)
        return (grad_q_all, grad_k_all, grad_v_all)

    init = (
        jnp.zeros(query.shape, jnp.float32),
        jnp.zeros(keys_all.shape, jnp.float32),
        jnp.zeros(values_all.shape, jnp.float32),
    )
    return lax.fori_loop(0, head_count // per_group, group_step, init)


def local(
    inputs,
    block_of,
    first_gain,
    first_shift,
    w_qkv,
    qkv_bias,
    w_out,
    second_gain,
    second_shift,
    w_gateup,
    w_down,
    cotangent,
):
    block_rows = inputs.shape[2]
    tok_count = inputs.shape[1] * block_rows
    model_width = inputs.shape[3]
    token_rows = inputs.reshape(tok_count, model_width).astype(jnp.float32)
    offsets = jnp.arange(block_rows, dtype=jnp.int32)
    local_pos = (block_of.reshape(-1)[:, None] * block_rows + offsets[None, :]).reshape(tok_count)
    cosine, sine_part = rotary_tables(local_pos)
    head_shape = (tok_count, HEADS, HEAD_DIM)
    full_qkv, full_out, gain_one, shift_one, bias_full = (
        lax.all_gather(w_qkv, "dp", axis=0, tiled=True),
        lax.all_gather(w_out, "dp", axis=0, tiled=True),
        lax.all_gather(first_gain.astype(jnp.bfloat16), "dp", axis=0, tiled=True).astype(
            first_gain.dtype
        ),
        lax.all_gather(first_shift.astype(jnp.bfloat16), "dp", axis=0, tiled=True).astype(
            first_shift.dtype
        ),
        lax.all_gather(qkv_bias.astype(jnp.bfloat16), "dp", axis=0, tiled=True).astype(
            qkv_bias.dtype
        ),
    )
    normed_out, normed_one, inverse_one = layer_norm(token_rows, gain_one, shift_one)
    hidden_one = normed_out.astype(jnp.bfloat16)
    projected = jnp.dot(hidden_one, full_qkv, preferred_element_type=jnp.float32) + bias_full
    query = rotate_heads(
        projected[:, :model_width].reshape(head_shape), cosine, sine_part, 1.0
    ).astype(jnp.bfloat16)
    keys_flat = (
        rotate_heads(
            projected[:, model_width : 2 * model_width].reshape(head_shape), cosine, sine_part, 1.0
        )
        .reshape(tok_count, model_width)
        .astype(jnp.bfloat16)
    )
    values_flat = projected[:, 2 * model_width :].astype(jnp.bfloat16)
    keys_gathered, values_gathered, blocks_gathered = (
        lax.all_gather(keys_flat, "ctx", axis=0, tiled=True),
        lax.all_gather(values_flat, "ctx", axis=0, tiled=True),
        lax.all_gather(block_of, "ctx", axis=1, tiled=True),
    )
    seq_rows = keys_gathered.shape[0]
    key_pos = (blocks_gathered.reshape(-1)[:, None] * block_rows + offsets[None, :]).reshape(
        seq_rows
    )
    key_shape = (seq_rows, HEADS, HEAD_DIM)
    attended, log_totals = attend(
        query,
        keys_gathered.reshape(key_shape),
        values_gathered.reshape(key_shape),
        local_pos,
        key_pos,
    )
    attended_flat = attended.reshape(tok_count, model_width)
    middle = token_rows + jnp.dot(attended_flat, full_out, preferred_element_type=jnp.float32)
    full_gateup, full_down, gain_two, shift_two = (
        lax.all_gather(w_gateup, "dp", axis=0, tiled=True),
        lax.all_gather(w_down, "dp", axis=0, tiled=True),
        lax.all_gather(second_gain.astype(jnp.bfloat16), "dp", axis=0, tiled=True).astype(
            second_gain.dtype
        ),
        lax.all_gather(second_shift.astype(jnp.bfloat16), "dp", axis=0, tiled=True).astype(
            second_shift.dtype
        ),
    )
    normed_out_two, normed_two, inverse_two = layer_norm(middle, gain_two, shift_two)
    hidden_two = normed_out_two.astype(jnp.bfloat16)
    gate_up = jnp.dot(hidden_two, full_gateup, preferred_element_type=jnp.float32)
    hidden_units = full_down.shape[0]
    gate_part = gate_up[:, :hidden_units]
    up_part = gate_up[:, hidden_units:]
    sigmoid_gate = jax.nn.sigmoid(gate_part)
    activation = (gate_part * sigmoid_gate * up_part).astype(jnp.bfloat16)
    result = middle + jnp.dot(activation, full_down, preferred_element_type=jnp.float32)
    outputs = result.astype(jnp.bfloat16).reshape(inputs.shape)
    grad_rows = cotangent.reshape(tok_count, model_width)
    grad_act = jnp.einsum("td,fd->tf", grad_rows, full_down, preferred_element_type=jnp.float32)
    grad_gate = grad_act * up_part * sigmoid_gate * (1.0 + gate_part * (1.0 - sigmoid_gate))
    grad_up = grad_act * gate_part * sigmoid_gate
    grad_gu = jnp.concatenate([grad_gate, grad_up], axis=1).astype(jnp.bfloat16)
    grad_hidden_two = jnp.einsum(
        "tf,df->td", grad_gu, full_gateup, preferred_element_type=jnp.float32
    )
    gain_two_term = jnp.sum(grad_hidden_two * normed_two, axis=0)
    shift_two_term = jnp.sum(grad_hidden_two, axis=0)
    grad_middle = grad_rows.astype(jnp.float32) + norm_back(
        grad_hidden_two, normed_two, inverse_two, gain_two
    )
    grad_gateup = jnp.einsum("td,tf->df", hidden_two, grad_gu, preferred_element_type=jnp.float32)
    grad_down = jnp.einsum("tf,td->fd", activation, grad_rows, preferred_element_type=jnp.float32)
    mlp_shards = (
        lax.psum_scatter(
            grad_gateup.astype(jnp.bfloat16), "dp", scatter_dimension=0, tiled=True
        ).astype(jnp.float32),
        lax.psum_scatter(
            grad_down.astype(jnp.bfloat16), "dp", scatter_dimension=0, tiled=True
        ).astype(jnp.float32),
        lax.psum_scatter(
            gain_two_term.astype(jnp.bfloat16), "dp", scatter_dimension=0, tiled=True
        ).astype(jnp.float32),
        lax.psum_scatter(
            shift_two_term.astype(jnp.bfloat16), "dp", scatter_dimension=0, tiled=True
        ).astype(jnp.float32),
    )
    mlp_grads = (
        lax.psum(mlp_shards[0].astype(jnp.bfloat16), "ctx").astype(jnp.float32),
        lax.psum(mlp_shards[1].astype(jnp.bfloat16), "ctx").astype(jnp.float32),
        lax.psum(mlp_shards[2].astype(jnp.bfloat16), "ctx").astype(jnp.float32),
        lax.psum(mlp_shards[3].astype(jnp.bfloat16), "ctx").astype(jnp.float32),
    )
    full_qkv_again, full_out_again, gain_again = (
        lax.all_gather(w_qkv, "dp", axis=0, tiled=True),
        lax.all_gather(w_out, "dp", axis=0, tiled=True),
        lax.all_gather(first_gain.astype(jnp.bfloat16), "dp", axis=0, tiled=True).astype(
            first_gain.dtype
        ),
    )
    grad_middle_low = grad_middle.astype(jnp.bfloat16)
    grad_attended = jnp.einsum(
        "te,de->td", grad_middle_low, full_out_again, preferred_element_type=jnp.float32
    ).astype(jnp.bfloat16)
    grad_query, grad_keys_all, grad_values_all = attend_back(
        query,
        keys_gathered.reshape(key_shape),
        values_gathered.reshape(key_shape),
        attended,
        grad_attended.reshape(head_shape),
        log_totals,
        local_pos,
        key_pos,
    )
    grad_keys, grad_values = (
        lax.psum_scatter(
            grad_keys_all.reshape(seq_rows, model_width).astype(jnp.bfloat16),
            "ctx",
            scatter_dimension=0,
            tiled=True,
        ).astype(jnp.float32),
        lax.psum_scatter(
            grad_values_all.reshape(seq_rows, model_width).astype(jnp.bfloat16),
            "ctx",
            scatter_dimension=0,
            tiled=True,
        ).astype(jnp.float32),
    )
    grad_query_plain = rotate_heads(grad_query, cosine, sine_part, -1.0).reshape(
        tok_count, model_width
    )
    grad_keys_plain = rotate_heads(grad_keys.reshape(head_shape), cosine, sine_part, -1.0).reshape(
        tok_count, model_width
    )
    grad_proj = jnp.concatenate([grad_query_plain, grad_keys_plain, grad_values], axis=1)
    grad_proj_low = grad_proj.astype(jnp.bfloat16)
    grad_hidden_one = jnp.einsum(
        "tf,df->td", grad_proj_low, full_qkv_again, preferred_element_type=jnp.float32
    )
    bias_term = jnp.sum(grad_proj, axis=0)
    gain_one_term = jnp.sum(grad_hidden_one * normed_one, axis=0)
    shift_one_term = jnp.sum(grad_hidden_one, axis=0)
    grad_inputs = grad_middle + norm_back(grad_hidden_one, normed_one, inverse_one, gain_again)
    grad_wout = jnp.einsum(
        "td,te->de", attended_flat, grad_middle_low, preferred_element_type=jnp.float32
    )
    grad_wqkv = jnp.einsum(
        "td,tf->df", hidden_one, grad_proj_low, preferred_element_type=jnp.float32
    )
    attn_shards = (
        lax.psum_scatter(
            grad_wqkv.astype(jnp.bfloat16), "dp", scatter_dimension=0, tiled=True
        ).astype(jnp.float32),
        lax.psum_scatter(
            bias_term.astype(jnp.bfloat16), "dp", scatter_dimension=0, tiled=True
        ).astype(jnp.float32),
        lax.psum_scatter(
            grad_wout.astype(jnp.bfloat16), "dp", scatter_dimension=0, tiled=True
        ).astype(jnp.float32),
        lax.psum_scatter(
            gain_one_term.astype(jnp.bfloat16), "dp", scatter_dimension=0, tiled=True
        ).astype(jnp.float32),
        lax.psum_scatter(
            shift_one_term.astype(jnp.bfloat16), "dp", scatter_dimension=0, tiled=True
        ).astype(jnp.float32),
    )
    attn_grads = (
        lax.psum(attn_shards[0].astype(jnp.bfloat16), "ctx").astype(jnp.float32),
        lax.psum(attn_shards[1].astype(jnp.bfloat16), "ctx").astype(jnp.float32),
        lax.psum(attn_shards[2].astype(jnp.bfloat16), "ctx").astype(jnp.float32),
        lax.psum(attn_shards[3].astype(jnp.bfloat16), "ctx").astype(jnp.float32),
        lax.psum(attn_shards[4].astype(jnp.bfloat16), "ctx").astype(jnp.float32),
    )
    results = (
        attn_grads[3],
        attn_grads[4],
        attn_grads[0],
        attn_grads[1],
        attn_grads[2],
        mlp_grads[2],
        mlp_grads[3],
        mlp_grads[0],
        mlp_grads[1],
    )
    return (outputs, grad_inputs.reshape(inputs.shape)) + results


def solution(mesh):
    placed = (
        P("dp", "ctx", None, None),
        P("dp", "ctx"),
        P("dp"),
        P("dp"),
        P("dp", None),
        P("dp"),
        P("dp", None),
        P("dp"),
        P("dp"),
        P("dp", None),
        P("dp", None),
        P("dp", "ctx", None, None),
    )
    return jax.shard_map(
        local,
        mesh=mesh,
        in_specs=placed,
        out_specs=(
            P("dp", "ctx", None, None),
            P("dp", "ctx", None, None),
            P("dp"),
            P("dp"),
            P("dp", None),
            P("dp"),
            P("dp", None),
            P("dp"),
            P("dp"),
            P("dp", None),
            P("dp", None),
        ),
        check_vma=False,
    )
```

profile of v0, /device:TPU:0, one launch (start us, length us, event | category | flops | bytes accessed | tf_op | source)
XLA Modules:
  0.0 2973.1 jit_solution(4743477724046858579)
XLA Ops:
  8.0 9.6 all-gather.1
  17.7 8.1 all-gather
  25.8 7.6 all-gather.2
  34.6 205.7 %all-gather.12.cloned.1.call-done = bf16[2048,6144]{1,0:T(8,128)(2,1)} async-done(((bf16[512,6144]{1,0:T(8,128)(2,1)}), bf16[2048,6144]{1,0:T(8,128)(2,1)}) %all-gather.12.cloned.1.call-update) | async-done | bytes 25165840 | tf_op jit(solution)/shard_map/all_gather | solution.py:158
  240.3 11.6 convolution_add_fusion
  271.3 8.2 all-gather.4
  279.5 7.0 all-gather.3
  287.9 9.8 all-reduce
  299.5 38.6 %all-gather.14.cloned.1.call-done = bf16[2048,2048]{1,0:T(8,128)(2,1)} async-done(((bf16[256,2048]{1,0:T(8,128)(2,1)}), bf16[2048,2048]{1,0:T(8,128)(2,1)}) %all-gather.14.cloned.1.call-update) | async-done | bytes 8388624 | tf_op jit(solution)/shard_map/all_gather | solution.py:186
  338.1 12.3 copy.38
  350.4 70.9 %all-gather.16.cloned.1.call-done = bf16[2048,2048]{0,1:T(8,128)(2,1)} async-done(((bf16[256,2048]{0,1:T(8,128)(2,1)}), bf16[2048,2048]{0,1:T(8,128)(2,1)}) %all-gather.16.cloned.1.call-update) | async-done | bytes 8388624 | tf_op jit(solution)/shard_map/all_gather | solution.py:185
  421.5 72.2 %while.34 = (s32[]{:T(128)}, bf16[256,32,64]{0,2,1:T(8,128)(2,1)S(1)}, f32[32,256]{1,0:T(8,128)S(1)}, bf16[2048,32,64]{0,2,1:T(8,128)(2,1)}, bf16[256,32,64]{0,2...) while((s32[]{:T(128)}, ...), condition=%wide.region_5.6_spmd.clone, body=%wide.region_2.5_spmd.clone.sunk | while | flops 560528384 | bytes 29666480 | solution.py:79
  493.7 15.1 all-gather.18.cloned.1.call-done
  508.7 6.2 fusion.64
  515.3 397.2 %all-gather.20.cloned.1.call-done = bf16[2048,11264]{1,0:T(8,128)(2,1)} async-done(((bf16[512,11264]{1,0:T(8,128)(2,1)}), bf16[2048,11264]{1,0:T(8,128)(2,1)}) %all-gather.20.cloned.1.call-update) | async-done | bytes 46137360 | tf_op jit(solution)/shard_map/all_gather | solution.py:204
  912.5 28.4 fusion.62
  940.9 183.7 %all-gather.22.cloned.1.call-done = bf16[5632,2048]{1,0:T(8,128)(2,1)} async-done(((bf16[1408,2048]{1,0:T(8,128)(2,1)}), bf16[5632,2048]{1,0:T(8,128)(2,1)}) %all-gather.22.cloned.1.call-update) | async-done | bytes 23068688 | tf_op jit(solution)/shard_map/all_gather | solution.py:205
  1124.5 26.0 multiply_convert_fusion.2
  1150.6 22.1 multiply_reduce_fusion
  1176.4 6.8 convolution_convert_fusion.4
  1188.7 4.5 broadcast.231
  1197.5 142.9 %while.35 = (s32[]{:T(128)}, f32[256,32,64]{0,2,1:T(8,128)}, bf16[2048,32,64]{0,2,1:T(8,128)(2,1)}, bf16[2048,32,64]{0,2,1:T(8,128)(2,1)}, bf16[2048,32,64]{0,2,...) while((s32[]{:T(128)}, f32[256,32,64]{0,2,1:T(8,128)}, ...), condition=%wide.region_11.12_spmd.clone, body=%wide.region_10.11_spmd.clone.sunk | while | flops 1364262912 | bytes 47491280 | solution.py:132
  1200.7 4.5 multiply_convert_fusion.5
  1218.6 4.5 multiply_convert_fusion.5
  1236.4 4.5 multiply_convert_fusion.5
  1254.2 4.5 multiply_convert_fusion.5
  1272.1 4.5 multiply_convert_fusion.5
  1289.9 4.5 multiply_convert_fusion.5
  1307.7 4.5 multiply_convert_fusion.5
  1325.5 4.5 multiply_convert_fusion.5
  1341.2 7.5 convolution_convert_fusion.3
  1349.9 13.4 convolution_convert_fusion.1
  1366.2 63.9 %reduce-scatter.7.cloned.1.call-done = bf16[256,2048]{0,1:T(8,128)(2,1)} async-done(((bf16[2048,2048]{0,1:T(8,128)(2,1)}), bf16[256,2048]{0,1:T(8,128)(2,1)}) %reduce-scatter.7.cloned.1.call-update) | async-done | bytes 1048592 | tf_op jit(solution)/shard_map/reduce_scatter | solution.py:280
  1434.3 86.1 %reduce-scatter.9.cloned.1.call-done = bf16[256,2048]{0,1:T(8,128)(2,1)} async-done(((bf16[2048,2048]{0,1:T(8,128)(2,1)}), bf16[256,2048]{0,1:T(8,128)(2,1)}) %reduce-scatter.9.cloned.1.call-update) | async-done | bytes 1048592 | tf_op jit(solution)/shard_map/reduce_scatter | solution.py:286
  1527.2 13.6 convolution_convert_fusion.2
  1541.5 21.6 convolution_convert_fusion
  1563.2 45.7 %reduce-scatter.13.cloned.1.call-done = bf16[512,2048]{1,0:T(8,128)(2,1)} async-done(((bf16[2048,2048]{1,0:T(8,128)(2,1)}), bf16[512,2048]{1,0:T(8,128)(2,1)}) %reduce-scatter.13.cloned.1.call-update) | async-done | bytes 2097168 | tf_op jit(solution)/shard_map/reduce_scatter | solution.py:321
  1608.9 208.3 %reduce-scatter.17.cloned.1.call-done = bf16[1408,2048]{1,0:T(8,128)(2,1)} async-done(((bf16[5632,2048]{1,0:T(8,128)(2,1)}), bf16[1408,2048]{1,0:T(8,128)(2,1)}) %reduce-scatter.17.cloned.1.call-update) | async-done | bytes 5767184 | tf_op jit(solution)/shard_map/reduce_scatter | solution.py:242
  1817.2 224.9 %reduce-scatter.11.cloned.1.call-done = bf16[512,6144]{1,0:T(8,128)(2,1)} async-done(((bf16[2048,6144]{1,0:T(8,128)(2,1)}), bf16[512,6144]{1,0:T(8,128)(2,1)}) %reduce-scatter.11.cloned.1.call-update) | async-done | bytes 6291472 | tf_op jit(solution)/shard_map/reduce_scatter | solution.py:315
  2042.0 393.1 %reduce-scatter.15.cloned.1.call-done = bf16[512,11264]{1,0:T(8,128)(2,1)} async-done(((bf16[2048,11264]{1,0:T(8,128)(2,1)}), bf16[512,11264]{1,0:T(8,128)(2,1)}) %reduce-scatter.15.cloned.1.call-update) | async-done | bytes 11534352 | tf_op jit(solution)/shard_map/reduce_scatter | solution.py:239
  2437.7 14.1 fusion.50
  2453.8 14.3 multiply_reduce_fusion.1
  2468.1 15.4 all-reduce.8
  2484.0 15.0 all-reduce.6
  2506.3 432.8 %all-reduce.11.cloned.1.call-done = (bf16[512,6144]{1,0:T(8,128)(2,1)}, bf16[512,2048]{1,0:T(8,128)(2,1)}, bf16[512,11264]{1,0:T(8,128)(2,1)}, bf16[1408,2048]{1,0:T(8,128)(2,1)}) async-done(((bf16[512,6144]{1,0:T(8,128)(2,1)}, bf16[512,2048]{1,0:T(8,128)(2,1)}, bf16[512,11264]{1,0:T(8,128)(2,1)}, bf16[1408,2048]{1,0:T(8,128)(2,1)}), (bf16[512,6144]{1,0:T(8,128)(2,1)}, bf16[512,2048]{1,0:T(8,128)(2,1)}, ...) | async-done | bytes 25690128 | tf_op jit(solution)/shard_map/psum | solution.py:332
  2939.1 10.1 convert_element_type.234
  2951.9 8.3 convert_element_type.244
  2960.1 6.0 convert_element_type.246
  (275 shorter events, 246.0 us)
Async XLA Ops:
  7.2 10.4 copy-start.36
  7.2 18.5 copy-start.32
  7.2 26.2 copy-start
  7.2 233.1 %all-gather.12.cloned.1.call-start = ((), (), s32[]{:S(2)}) async-start(), calls=%async_computation.6 | async-start | bytes 31457280 | tf_op jit(solution)/shard_map/all_gather | solution.py:158
  8.0 330.2 %all-gather.14.cloned.1.call-start = ((), (), s32[]{:S(2)}) async-start(), calls=%async_computation.7 | async-start | bytes 9437184 | tf_op jit(solution)/shard_map/all_gather | solution.py:186
  25.7 226.2 %copy-start.25 = (f32[4,1,512]{2,1,0:T(1,128)}, f32[4,1,512]{2,1,0:T(1,128)S(1)}, u32[]{:S(2)}) copy-start(f32[4,1,512]{2,1,0:T(1,128)S(1)} %convert_element_type.248) | copy-start | bytes 24580
  33.7 218.3 %copy-start.28 = (f32[256]{0:T(256)}, f32[256]{0:T(256)S(1)}, u32[]{:S(2)}) copy-start(f32[256]{0:T(256)S(1)} %get-tuple-element.483) | copy-start | bytes 3076
  34.1 217.8 %copy-start.30 = (f32[256]{0:T(256)}, f32[256]{0:T(256)S(1)}, u32[]{:S(2)}) copy-start(f32[256]{0:T(256)S(1)} %rsqrt_bitcast_fusion) | copy-start | bytes 3076
  34.6 217.3 %copy-start.15 = (bf16[256,2048]{1,0:T(8,128)(2,1)}, bf16[256,2048]{1,0:T(8,128)(2,1)S(1)}, u32[]{:S(2)}) copy-start(bf16[256,2048]{1,0:T(8,128)(2,1)S(1)} %add_convert_fusion.1) | copy-start | bytes 3145732
  251.9 2.7 copy-start.17
  255.8 165.5 %all-gather.16.cloned.1.call-start = ((), (), s32[]{:S(2)}) async-start(), calls=%async_computation.8 | async-start | bytes 9437184 | tf_op jit(solution)/shard_map/all_gather | solution.py:185
  256.7 10.3 copy-start.23
  269.4 239.3 %all-gather.18.cloned.1.call-start = ((), (), s32[]{:S(2)}) async-start(), calls=%async_computation.9 | async-start | bytes 10485760 | tf_op jit(solution)/shard_map/all_gather | solution.py:159
  270.0 642.5 %all-gather.20.cloned.1.call-start = ((), (), s32[]{:S(2)}) async-start(), calls=%async_computation.10 | async-start | bytes 57671680 | tf_op jit(solution)/shard_map/all_gather | solution.py:204
  270.6 8.9 copy-start.38
  270.6 16.0 copy-start.41
  270.6 853.9 %all-gather.22.cloned.1.call-start = ((), (), s32[]{:S(2)}) async-start(), calls=%async_computation.11 | async-start | bytes 28835840 | tf_op jit(solution)/shard_map/all_gather | solution.py:205
  271.2 1158.9 %reduce-scatter.7.cloned.1.call-start = ((), (), s32[]{:S(2)}) async-start(), calls=%async_computation.12 | async-start | bytes 9437184 | tf_op jit(solution)/shard_map/reduce_scatter | solution.py:280
  279.5 633.0 %copy-start.21 = (f32[4,1,512]{2,1,0:T(1,128)}, f32[4,1,512]{2,1,0:T(1,128)S(1)}, u32[]{:S(2)}) copy-start(f32[4,1,512]{2,1,0:T(1,128)S(1)} %convert_element_type.252) | copy-start | bytes 24580
  493.6 15.1 copy-start.2
  493.6 15.1 copy-start.11
  912.5 212.1 %copy-start.18 = (bf16[1,2,128,2048]{3,2,1,0:T(8,128)(2,1)S(1)}, bf16[1,2,128,2048]{3,2,1,0:T(8,128)(2,1)}, u32[]{:S(2)}) copy-start(bf16[1,2,128,2048]{3,2,1,0:T(8,128)(2,1)} %param.27) | copy-start | bytes 3145732
  1176.4 9.1 copy-start.3
  1340.4 180.0 %reduce-scatter.9.cloned.1.call-start = ((), (), s32[]{:S(2)}) async-start(), calls=%async_computation.13 | async-start | bytes 9437184 | tf_op jit(solution)/shard_map/reduce_scatter | solution.py:286
  1341.2 267.7 %reduce-scatter.13.cloned.1.call-start = ((), (), s32[]{:S(2)}) async-start(), calls=%async_computation.15 | async-start | bytes 10485760 | tf_op jit(solution)/shard_map/reduce_scatter | solution.py:321
  1348.7 468.4 %reduce-scatter.17.cloned.1.call-start = ((), (), s32[]{:S(2)}) async-start(), calls=%async_computation.17 | async-start | bytes 28835840 | tf_op jit(solution)/shard_map/reduce_scatter | solution.py:242
  1363.4 678.6 %reduce-scatter.11.cloned.1.call-start = ((), (), s32[]{:S(2)}) async-start(), calls=%async_computation.14 | async-start | bytes 31457280 | tf_op jit(solution)/shard_map/reduce_scatter | solution.py:315
  1430.1 2.6 copy-start.12
  1432.7 89.3 %copy-start.24 = (f32[256,8]{0,1:T(8,128)S(1)}, f32[256,8]{0,1:T(8,128)}, u32[]{:S(2)}) copy-start(f32[256,8]{0,1:T(8,128)} %copy-done.23) | copy-start | bytes 24580
  1432.7 89.3 %copy-start.27 = (f32[256,8]{0,1:T(8,128)S(1)}, f32[256,8]{0,1:T(8,128)}, u32[]{:S(2)}) copy-start(f32[256,8]{0,1:T(8,128)} %get-tuple-element.480) | copy-start | bytes 24580
  1520.4 3.6 copy-start.14
  1521.9 5.1 copy-start.4
  1522.0 3.6 copy-start.13
  1540.8 894.4 %reduce-scatter.15.cloned.1.call-start = ((), (), s32[]{:S(2)}) async-start(), calls=%async_computation.16 | async-start | bytes 57671680 | tf_op jit(solution)/shard_map/reduce_scatter | solution.py:239
  1563.1 1375.9 %all-reduce.11.cloned.1.call-start = ((), (), s32[]{:S(2)}) async-start(), calls=%async_computation.18 | async-start | bytes 51380224 | tf_op jit(solution)/shard_map/psum | solution.py:332
  2437.7 14.1 copy-start.5
  2437.7 14.1 copy-start.7
  2437.7 14.1 copy-start.8
  2451.8 1.9 copy-start.6
  2451.9 1.9 copy-start.26
  2451.9 1.9 copy-start.29
  2451.9 1.9 copy-start.31
  2453.8 14.4 copy-start.33
  2453.8 14.4 copy-start.34
  2939.1 10.1 copy-start.20
  2939.1 12.8 copy-start.10
  2949.2 10.9 slice-start
  2951.9 8.3 slice-start.1
  (9 other events, 10.1 us)
Sparse Core Ops, SparseCore 0:
  9.9 230.3 all-gather.11
  255.9 82.1 all-gather.13
  340.3 80.9 all-gather.15
  423.0 85.6 all-gather.17
  510.4 401.9 all-gather.19
  914.2 210.3 all-gather.21
  1340.5 89.5 reduce-scatter.6
  1432.4 88.0 reduce-scatter.8
  1524.1 84.7 reduce-scatter.12
  1612.4 204.7 reduce-scatter.16
  1820.3 221.6 reduce-scatter.10
  2045.0 390.0 reduce-scatter.14
  2438.0 500.9 all-reduce.10
where the time goes:
time: 2980 us; the launch traced here: 2970 us
  waiting for transfers between devices  2370 us (80%)
  matrix products  376 us (13%)
  blocking collectives  80.8 us (3%)
  other arithmetic  76.8 us (3%)
  local copies, waits for them, and re-layouts  51.8 us (2%)
    psum x1, waiting for transfers between devices, local(): lax.psum(attn_shards[0].astype(jnp.bfloat16), 'ctx').astype(jnp.float32)  433 us
    all_gather x1, waiting for transfers between devices, local(): lax.all_gather(w_gateup, 'dp', axis=0, tiled=True)  397 us
    reduce_scatter x1, waiting for transfers between devices, local(): lax.psum_scatter(grad_gateup.astype(jnp.bfloat16), 'dp', scatter_dimensio...  393 us
    reduce_scatter x1, waiting for transfers between devices, local(): lax.psum_scatter(grad_wqkv.astype(jnp.bfloat16), 'dp', scatter_dimension=...  225 us
    reduce_scatter x1, waiting for transfers between devices, local(): lax.psum_scatter(grad_down.astype(jnp.bfloat16), 'dp', scatter_dimension=...  208 us
    all_gather x1, waiting for transfers between devices, local(): lax.all_gather(w_qkv, 'dp', axis=0, tiled=True)  206 us
    all_gather x1, waiting for transfers between devices, local(): lax.all_gather(w_down, 'dp', axis=0, tiled=True)  184 us
    reduce_scatter x1, waiting for transfers between devices, local(): lax.psum_scatter(grad_values_all.reshape(seq_rows, model_width).astype(jn...  86.1 us
  transfers between devices with their start and end apart: 13, of which 13 were waited for; matrix products, arithmetic and copies ran while one was open for 8% of the time, Pallas kernels for 0%

commit v1 on v0

--- a/solution.py
+++ b/solution.py
@@ -7,6 +7,31 @@
 HEAD_DIM = 64
 ROT = 16
 epsilon = 1e-05
+
+
+def produce_classes(field_in, where_dim):
+    field_in = jnp.moveaxis(field_in, 0, where_dim)
+    shaped = field_in.shape
+    return field_in.reshape(
+        *shaped[:where_dim], shaped[where_dim] * shaped[where_dim + 1], *shaped[where_dim + 2 :]
+    )
+
+
+def _replace_scales(xs, ax_name, d0):
+    world = jax.lax.axis_size(ax_name)
+    stack_in = list(map(lambda ix: (ix, (ix + 1) % world), range(world)))
+    b_next, v1 = ([], [])
+    heap = [(num, to_i) for to_i, num in stack_in]
+    for idx in [*range(world - 1)]:
+        if idx % 2 == 0:
+            b_next.append(jax.lax.ppermute(b_next[-1] if b_next else xs, ax_name, stack_in))
+        else:
+            later = jax.lax.ppermute(v1[-1] if v1 else xs, ax_name, heap)
+            v1.append(later)
+    oldest = jnp.stack([*b_next[::-1], xs, *v1])
+    low = jax.lax.axis_index(ax_name) - len(b_next)
+    oldest = oldest[(jnp.arange(world) - low) % world]
+    return produce_classes(oldest, d0)
 
 
 def layer_norm(token_rows, gain_vec, shift_vec):
@@ -155,7 +180,7 @@
     cosine, sine_part = rotary_tables(local_pos)
     head_shape = (tok_count, HEADS, HEAD_DIM)
     full_qkv, full_out, gain_one, shift_one, bias_full = (
-        lax.all_gather(w_qkv, "dp", axis=0, tiled=True),
+        _replace_scales(w_qkv, "dp", 0),
         lax.all_gather(w_out, "dp", axis=0, tiled=True),
         lax.all_gather(first_gain.astype(jnp.bfloat16), "dp", axis=0, tiled=True).astype(
             first_gain.dtype

time: 2980 us -> 3490 us (1.17)
  blocking collectives: 80.8 us -> 343 us
  waiting for transfers between devices: 2370 us -> 2520 us
  other arithmetic: 76.8 us -> 123 us
  local copies, waits for them, and re-layouts: 51.8 us -> 96.5 us
    all_gather x1, blocking collectives: 9.57 us -> 269 us  [local(): lax.all_gather(first_shift.astype(jnp.bfloat16), 'dp', axis=0, tiled=True)]
    ppermute x0 -> x3, waiting for transfers between devices: none -> 137 us  [the longest x2 137 us: _replace_scales(): jax.lax.ppermute(b_next[-1] if b_next else xs, ax_name, stack_in)]
    gather x0 -> x5, local copies, waits for them, and re-layouts: none -> 43.7 us  [_replace_scales(): oldest = oldest[(jnp.arange(world) - low) % world]]
  transfers between devices with their start and end apart: 13 -> 16, of which waited for: 13 -> 14; matrix products, arithmetic and copies ran while one was open for 8% -> 7% of each run, Pallas kernels for 0% -> 0%
where the time goes in v1:
time: 3490 us; the launch traced here: 3480 us
  waiting for transfers between devices  2520 us (72%)
  matrix products  370 us (11%)
  blocking collectives  343 us (10%)
  other arithmetic  123 us (4%)
  local copies, waits for them, and re-layouts  96.5 us (3%)
    psum x1, waiting for transfers between devices, local(): lax.psum(attn_shards[0].astype(jnp.bfloat16), 'ctx').astype(jnp.float32)  448 us
    all_gather x1, waiting for transfers between devices, local(): lax.all_gather(w_gateup, 'dp', axis=0, tiled=True)  397 us
    reduce_scatter x1, waiting for transfers between devices, local(): lax.psum_scatter(grad_gateup.astype(jnp.bfloat16), 'dp', scatter_dimensio...  393 us
    all_gather x1, blocking collectives, local(): lax.all_gather(first_shift.astype(jnp.bfloat16), 'dp', axis=0, tiled=True)  269 us
    reduce_scatter x1, waiting for transfers between devices, local(): lax.psum_scatter(grad_wqkv.astype(jnp.bfloat16), 'dp', scatter_dimension=...  225 us
    all_gather x1, waiting for transfers between devices, local(): lax.all_gather(w_qkv, 'dp', axis=0, tiled=True)  220 us
    reduce_scatter x1, waiting for transfers between devices, local(): lax.psum_scatter(grad_down.astype(jnp.bfloat16), 'dp', scatter_dimension=...  208 us
    all_gather x1, waiting for transfers between devices, local(): lax.all_gather(w_down, 'dp', axis=0, tiled=True)  184 us
  transfers between devices with their start and end apart: 16, of which 14 were waited for; matrix products, arithmetic and copies ran while one was open for 7% of the time, Pallas kernels for 0%

profile of v1, /device:TPU:0, one launch (start us, length us, event | category | flops | bytes accessed | tf_op | source)
XLA Modules:
  0.0 3476.3 jit_solution(16995201065497515441)
XLA Ops:
  11.3 136.6 %collective-permute-done = bf16[512,6144]{1,0:T(8,128)(2,1)} collective-permute-done((bf16[512,6144]{1,0:T(8,128)(2,1)}, bf16[512,6144]{1,0:T(8,128)(2,1)}, u32[]{:S(2)}, u32[]{:S(2)}) %collective-permute-start) | collective-permute-done | bytes 6291488 | tf_op jit(solution)/shard_map/ppermute | solution.py:27
  149.6 269.4 %all-gather.1 = bf16[4,1,512]{2,1,0:T(2,128)(2,1)S(1)} all-gather(bf16[1,1,512]{2,1,0:T(2,128)(2,1)S(1)} %reshape.419), channel_id=1, replica_groups=mesh['dp'=4,'ctx'=8] {'dp'}, dimensions={0}, use_global_device_ids=true | all-gather | bytes 5120 | tf_op jit(solution)/shard_map/all_gather | solution.py:188
  419.8 8.1 all-gather
  428.6 7.2 all-gather.2
  441.8 20.8 pad_maximum_fusion
  462.6 17.9 fusion.66
  480.5 6.4 gather_fusion.3
  486.9 6.4 gather_fusion.2
  493.4 6.4 gather_fusion.1
  499.8 6.4 gather_fusion
  506.2 17.4 pad_maximum_fusion.1
  523.7 11.6 convolution_add_fusion
  554.9 8.3 all-gather.4
  563.2 6.9 all-gather.3
  571.5 12.3 all-reduce
  585.5 36.3 %all-gather.12.cloned.1.call-done = bf16[2048,2048]{1,0:T(8,128)(2,1)} async-done(((bf16[256,2048]{1,0:T(8,128)(2,1)}), bf16[2048,2048]{1,0:T(8,128)(2,1)}) %all-gather.12.cloned.1.call-update) | async-done | bytes 8388624 | tf_op jit(solution)/shard_map/all_gather | solution.py:211
  621.8 12.3 copy.38
  634.1 70.9 %all-gather.14.cloned.1.call-done = bf16[2048,2048]{0,1:T(8,128)(2,1)} async-done(((bf16[256,2048]{0,1:T(8,128)(2,1)}), bf16[2048,2048]{0,1:T(8,128)(2,1)}) %all-gather.14.cloned.1.call-update) | async-done | bytes 8388624 | tf_op jit(solution)/shard_map/all_gather | solution.py:210
  705.1 72.2 %while.34 = (s32[]{:T(128)}, bf16[256,32,64]{0,2,1:T(8,128)(2,1)S(1)}, f32[32,256]{1,0:T(8,128)S(1)}, bf16[2048,32,64]{0,2,1:T(8,128)(2,1)}, bf16[256,32,64]{0,2...) while((s32[]{:T(128)}, ...), condition=%wide.region_5.6_spmd.clone, body=%wide.region_2.5_spmd.clone.sunk | while | flops 560528384 | bytes 29666480 | solution.py:104
  777.4 15.1 all-gather.16.cloned.1.call-done
  792.6 6.2 fusion.68
  799.1 397.2 %all-gather.18.cloned.1.call-done = bf16[2048,11264]{1,0:T(8,128)(2,1)} async-done(((bf16[512,11264]{1,0:T(8,128)(2,1)}), bf16[2048,11264]{1,0:T(8,128)(2,1)}) %all-gather.18.cloned.1.call-update) | async-done | bytes 46137360 | tf_op jit(solution)/shard_map/all_gather | solution.py:229
  1196.3 28.4 fusion.65
  1224.7 183.7 %all-gather.20.cloned.1.call-done = bf16[5632,2048]{1,0:T(8,128)(2,1)} async-done(((bf16[1408,2048]{1,0:T(8,128)(2,1)}), bf16[5632,2048]{1,0:T(8,128)(2,1)}) %all-gather.20.cloned.1.call-update) | async-done | bytes 23068688 | tf_op jit(solution)/shard_map/all_gather | solution.py:230
  1408.4 26.0 multiply_convert_fusion.2
  1434.4 22.2 multiply_reduce_fusion
  1460.5 5.8 convolution_convert_fusion.4
  1476.8 137.2 %while.35 = (s32[]{:T(128)}, f32[256,32,64]{0,2,1:T(8,128)S(1)}, bf16[2048,32,64]{0,2,1:T(8,128)(2,1)}, bf16[2048,32,64]{0,2,1:T(8,128)(2,1)}, bf16[2048,32,64]{...) while((s32[]{:T(128)}, f32[256,32,64]{0,2,1:T(8,128)S(1)}, ...), condition=%wide.region_11.12_spmd.clone, body=%wide.region_10.11_spmd.clone.sunk | while | flops 1364262912 | bytes 47491280 | solution.py:157
  1480.0 4.5 multiply_convert_fusion.5
  1617.0 5.8 convolution_convert_fusion.3
  1624.6 12.9 convolution_convert_fusion.1
  1640.4 63.4 %reduce-scatter.7.cloned.1.call-done = bf16[256,2048]{0,1:T(8,128)(2,1)} async-done(((bf16[2048,2048]{0,1:T(8,128)(2,1)}), bf16[256,2048]{0,1:T(8,128)(2,1)}) %reduce-scatter.7.cloned.1.call-update) | async-done | bytes 1048592 | tf_op jit(solution)/shard_map/reduce_scatter | solution.py:305
  1709.0 85.0 %reduce-scatter.9.cloned.1.call-done = bf16[256,2048]{0,1:T(8,128)(2,1)} async-done(((bf16[2048,2048]{0,1:T(8,128)(2,1)}), bf16[256,2048]{0,1:T(8,128)(2,1)}) %reduce-scatter.9.cloned.1.call-update) | async-done | bytes 1048592 | tf_op jit(solution)/shard_map/reduce_scatter | solution.py:311
  1802.2 219.8 %all-gather.22.cloned.1.call-done = bf16[2048,6144]{1,0:T(8,128)(2,1)} async-done(((bf16[512,6144]{1,0:T(8,128)(2,1)}), bf16[2048,6144]{1,0:T(8,128)(2,1)}) %all-gather.22.cloned.1.call-update) | async-done | bytes 25165840 | tf_op jit(solution)/shard_map/all_gather | solution.py:284
  2022.0 15.7 multiply_reduce_fusion.1
  2037.7 13.9 convolution_convert_fusion.2
  2053.3 22.4 convolution_convert_fusion
  2075.8 36.2 %reduce-scatter.13.cloned.1.call-done = bf16[512,2048]{1,0:T(8,128)(2,1)} async-done(((bf16[2048,2048]{1,0:T(8,128)(2,1)}), bf16[512,2048]{1,0:T(8,128)(2,1)}) %reduce-scatter.13.cloned.1.call-update) | async-done | bytes 2097168 | tf_op jit(solution)/shard_map/reduce_scatter | solution.py:346
  2112.0 208.3 %reduce-scatter.17.cloned.1.call-done = bf16[1408,2048]{1,0:T(8,128)(2,1)} async-done(((bf16[5632,2048]{1,0:T(8,128)(2,1)}), bf16[1408,2048]{1,0:T(8,128)(2,1)}) %reduce-scatter.17.cloned.1.call-update) | async-done | bytes 5767184 | tf_op jit(solution)/shard_map/reduce_scatter | solution.py:267
  2320.3 224.9 %reduce-scatter.11.cloned.1.call-done = bf16[512,6144]{1,0:T(8,128)(2,1)} async-done(((bf16[2048,6144]{1,0:T(8,128)(2,1)}), bf16[512,6144]{1,0:T(8,128)(2,1)}) %reduce-scatter.11.cloned.1.call-update) | async-done | bytes 6291472 | tf_op jit(solution)/shard_map/reduce_scatter | solution.py:340
  2545.1 393.1 %reduce-scatter.15.cloned.1.call-done = bf16[512,11264]{1,0:T(8,128)(2,1)} async-done(((bf16[2048,11264]{1,0:T(8,128)(2,1)}), bf16[512,11264]{1,0:T(8,128)(2,1)}) %reduce-scatter.15.cloned.1.call-update) | async-done | bytes 11534352 | tf_op jit(solution)/shard_map/reduce_scatter | solution.py:264
  2940.8 13.9 fusion.50
  2956.5 15.4 all-reduce.8
  2972.3 15.0 all-reduce.6
  2994.1 448.1 %all-reduce.11.cloned.1.call-done = (bf16[512,6144]{1,0:T(8,128)(2,1)}, bf16[512,2048]{1,0:T(8,128)(2,1)}, bf16[512,11264]{1,0:T(8,128)(2,1)}, bf16[1408,2048]{1,0:T(8,128)(2,1)}) async-done(((bf16[512,6144]{1,0:T(8,128)(2,1)}, bf16[512,2048]{1,0:T(8,128)(2,1)}, bf16[512,11264]{1,0:T(8,128)(2,1)}, bf16[1408,2048]{1,0:T(8,128)(2,1)}), (bf16[512,6144]{1,0:T(8,128)(2,1)}, bf16[512,2048]{1,0:T(8,128)(2,1)}, ...) | async-done | bytes 25690128 | tf_op jit(solution)/shard_map/psum | solution.py:357
  3442.1 10.2 convert_element_type.242
  3455.0 8.3 convert_element_type.252
  3463.3 6.0 convert_element_type.254
  (305 shorter events, 289.6 us)
Async XLA Ops:
  7.2 614.6 %all-gather.12.cloned.1.call-start = ((), (), s32[]{:S(2)}) async-start(), calls=%async_computation.6 | async-start | bytes 9437184 | tf_op jit(solution)/shard_map/all_gather | solution.py:211
  7.2 140.7 %collective-permute-start = (bf16[512,6144]{1,0:T(8,128)(2,1)}, bf16[512,6144]{1,0:T(8,128)(2,1)}, u32[]{:S(2)}, u32[]{:S(2)}) collective-permute-start(bf16[512,6144]{1,0:T(8,128)(2,1)} %param.20), channel_id=1, source_target_pairs={{0,8},{8,16},{16,24},{24,0},{1,9},{9,17},{17,25},{25,1},{2,10},{10... | collective-permute-start | bytes 18874376 | tf_op jit(solution)/shard_map/ppermute | solution.py:27
  10.2 431.5 %collective-permute-start.2 = (bf16[512,6144]{1,0:T(8,128)(2,1)}, bf16[512,6144]{1,0:T(8,128)(2,1)}, u32[]{:S(2)}, u32[]{:S(2)}) collective-permute-start(bf16[512,6144]{1,0:T(8,128)(2,1)} %param.20), channel_id=1, source_target_pairs={{8,0},{16,8},{24,16},{0,24},{9,1},{17,9},{25,17},{1,25},{10,2},{18... | collective-permute-start | bytes 18874376 | tf_op jit(solution)/shard_map/ppermute | solution.py:29
  147.9 293.9 %collective-permute-start.1 = (bf16[512,6144]{1,0:T(8,128)(2,1)}, bf16[512,6144]{1,0:T(8,128)(2,1)}, u32[]{:S(2)}, u32[]{:S(2)}) collective-permute-start(bf16[512,6144]{1,0:T(8,128)(2,1)} %collective-permute-done), channel_id=1, source_target_pairs={{0,8},{8,16},{16,24},{24,0},{1,9},{9,17},{17,25},{25,1},{2,10},{10... | collective-permute-start | bytes 18874376 | tf_op jit(solution)/shard_map/ppermute | solution.py:27
  419.1 43.5 %copy-start.35 = (f32[4,1,512]{2,1,0:T(1,128)}, f32[4,1,512]{2,1,0:T(1,128)S(1)}, u32[]{:S(2)}) copy-start(f32[4,1,512]{2,1,0:T(1,128)S(1)} %convert_element_type.257) | copy-start | bytes 24580
  427.9 34.7 copy-start.32
  523.7 15.5 copy-start.43
  539.2 165.8 %all-gather.14.cloned.1.call-start = ((), (), s32[]{:S(2)}) async-start(), calls=%async_computation.7 | async-start | bytes 9437184 | tf_op jit(solution)/shard_map/all_gather | solution.py:210
  540.0 10.4 copy-start.30
  552.9 239.7 %all-gather.16.cloned.1.call-start = ((), (), s32[]{:S(2)}) async-start(), calls=%async_computation.8 | async-start | bytes 10485760 | tf_op jit(solution)/shard_map/all_gather | solution.py:184
  553.6 642.7 %all-gather.18.cloned.1.call-start = ((), (), s32[]{:S(2)}) async-start(), calls=%async_computation.9 | async-start | bytes 57671680 | tf_op jit(solution)/shard_map/all_gather | solution.py:229
  554.2 9.0 copy-start.42
  554.2 15.9 copy-start.45
  554.2 854.1 %all-gather.20.cloned.1.call-start = ((), (), s32[]{:S(2)}) async-start(), calls=%async_computation.10 | async-start | bytes 28835840 | tf_op jit(solution)/shard_map/all_gather | solution.py:230
  554.8 1148.9 %reduce-scatter.7.cloned.1.call-start = ((), (), s32[]{:S(2)}) async-start(), calls=%async_computation.11 | async-start | bytes 9437184 | tf_op jit(solution)/shard_map/reduce_scatter | solution.py:305
  563.2 633.1 %copy-start.24 = (f32[4,1,512]{2,1,0:T(1,128)}, f32[4,1,512]{2,1,0:T(1,128)S(1)}, u32[]{:S(2)}) copy-start(f32[4,1,512]{2,1,0:T(1,128)S(1)} %convert_element_type.260) | copy-start | bytes 24580
  570.2 886.5 %copy-start.22 = (f32[4,1,512]{2,1,0:T(1,128)}, f32[4,1,512]{2,1,0:T(1,128)S(1)}, u32[]{:S(2)}) copy-start(f32[4,1,512]{2,1,0:T(1,128)S(1)} %convert_element_type.259) | copy-start | bytes 24580
  705.1 87.4 %copy-start.2 = (bf16[1,2,128,2048]{3,2,1,0:T(8,128)(2,1)S(1)}, bf16[1,2,128,2048]{3,2,1,0:T(8,128)(2,1)}, u32[]{:S(2)}) copy-start(bf16[1,2,128,2048]{3,2,1,0:T(8,128)(2,1)} %param.16) | copy-start | bytes 3145732
  777.4 15.2 copy-start.4
  777.4 15.2 copy-start.13
  798.7 657.9 %copy-start = (f32[256,2048]{1,0:T(8,128)}, f32[256,2048]{1,0:T(8,128)S(1)}, u32[]{:S(2)}) copy-start(f32[256,2048]{1,0:T(8,128)S(1)} %get-tuple-element.495) | copy-start | bytes 6291460
  798.7 657.9 %copy-start.26 = (f32[256]{0:T(256)}, f32[256]{0:T(256)S(1)}, u32[]{:S(2)}) copy-start(f32[256]{0:T(256)S(1)} %broadcast_multiply_fusion.5) | copy-start | bytes 3076
  799.1 657.6 %copy-start.28 = (f32[256]{0:T(256)}, f32[256]{0:T(256)S(1)}, u32[]{:S(2)}) copy-start(f32[256]{0:T(256)S(1)} %add_rsqrt_fusion) | copy-start | bytes 3076
  1196.3 212.1 %copy-start.19 = (bf16[1,2,128,2048]{3,2,1,0:T(8,128)(2,1)S(1)}, bf16[1,2,128,2048]{3,2,1,0:T(8,128)(2,1)}, u32[]{:S(2)}) copy-start(bf16[1,2,128,2048]{3,2,1,0:T(8,128)(2,1)} %param.27) | copy-start | bytes 3145732
  1614.0 180.0 %reduce-scatter.9.cloned.1.call-start = ((), (), s32[]{:S(2)}) async-start(), calls=%async_computation.12 | async-start | bytes 9437184 | tf_op jit(solution)/shard_map/reduce_scatter | solution.py:311
  1615.4 406.6 %all-gather.22.cloned.1.call-start = ((), (), s32[]{:S(2)}) async-start(), calls=%async_computation.13 | async-start | bytes 31457280 | tf_op jit(solution)/shard_map/all_gather | solution.py:284
  1616.2 495.8 %reduce-scatter.13.cloned.1.call-start = ((), (), s32[]{:S(2)}) async-start(), calls=%async_computation.15 | async-start | bytes 10485760 | tf_op jit(solution)/shard_map/reduce_scatter | solution.py:346
  1622.8 697.4 %reduce-scatter.17.cloned.1.call-start = ((), (), s32[]{:S(2)}) async-start(), calls=%async_computation.17 | async-start | bytes 28835840 | tf_op jit(solution)/shard_map/reduce_scatter | solution.py:267
  1637.5 907.6 %reduce-scatter.11.cloned.1.call-start = ((), (), s32[]{:S(2)}) async-start(), calls=%async_computation.14 | async-start | bytes 31457280 | tf_op jit(solution)/shard_map/reduce_scatter | solution.py:340
  1639.1 156.6 %copy-start.31 = (f32[256,8]{0,1:T(8,128)S(1)}, f32[256,8]{0,1:T(8,128)}, u32[]{:S(2)}) copy-start(f32[256,8]{0,1:T(8,128)} %copy-done.30) | copy-start | bytes 24580
  1639.1 156.6 %copy-start.34 = (f32[256,8]{0,1:T(8,128)S(1)}, f32[256,8]{0,1:T(8,128)}, u32[]{:S(2)}) copy-start(f32[256,8]{0,1:T(8,128)} %get-tuple-element.485) | copy-start | bytes 24580
  1795.6 242.2 %copy-start.6 = (f32[256,2048]{0,1:T(8,128)}, f32[256,2048]{0,1:T(8,128)S(1)}, u32[]{:S(2)}) copy-start(f32[256,2048]{0,1:T(8,128)S(1)} %convert_element_type.234) | copy-start | bytes 6291460
  1795.6 226.4 %copy-start.3 = (bf16[1,2,128,2048]{3,2,1,0:T(8,128)(2,1)S(1)}, bf16[1,2,128,2048]{3,2,1,0:T(8,128)(2,1)}, u32[]{:S(2)}) copy-start(bf16[1,2,128,2048]{3,2,1,0:T(8,128)(2,1)} %param.16) | copy-start | bytes 3145732
  1795.6 226.4 %copy-start.33 = (f32[4,1,512]{2,1,0:T(1,128)S(1)}, f32[4,1,512]{2,1,0:T(1,128)}, u32[]{:S(2)}) copy-start(f32[4,1,512]{2,1,0:T(1,128)} %copy-done.32) | copy-start | bytes 24580
  1795.6 226.4 %copy-start.36 = (f32[4,1,512]{2,1,0:T(1,128)S(1)}, f32[4,1,512]{2,1,0:T(1,128)}, u32[]{:S(2)}) copy-start(f32[4,1,512]{2,1,0:T(1,128)} %copy-done.35) | copy-start | bytes 24580
  1795.6 226.4 %copy-start.39 = (f32[256]{0:T(256)S(1)}, f32[256]{0:T(256)}, u32[]{:S(2)}) copy-start(f32[256]{0:T(256)} %get-tuple-element.490) | copy-start | bytes 3076
  1795.6 226.4 %copy-start.40 = (f32[256]{0:T(256)S(1)}, f32[256]{0:T(256)}, u32[]{:S(2)}) copy-start(f32[256]{0:T(256)} %get-tuple-element.488) | copy-start | bytes 3076
  2051.7 886.5 %reduce-scatter.15.cloned.1.call-start = ((), (), s32[]{:S(2)}) async-start(), calls=%async_computation.16 | async-start | bytes 57671680 | tf_op jit(solution)/shard_map/reduce_scatter | solution.py:264
  2075.7 1366.4 %all-reduce.11.cloned.1.call-start = ((), (), s32[]{:S(2)}) async-start(), calls=%async_computation.18 | async-start | bytes 51380224 | tf_op jit(solution)/shard_map/psum | solution.py:357
  2940.7 13.9 copy-start.7
  2940.8 13.9 copy-start.8
  2940.8 13.9 copy-start.9
  2954.7 35.6 %copy-start.12 = (f32[256,2048]{1,0:T(8,128)S(1)}, f32[256,2048]{1,0:T(8,128)}, u32[]{:S(2)}) copy-start(f32[256,2048]{1,0:T(8,128)} %copy-done.10) | copy-start | bytes 6291460
  3442.1 12.9 slice-start
  3442.1 10.2 copy-start.21
  3442.1 12.9 slice-start.1
  3442.1 12.9 slice-start.2
  3452.3 11.0 slice-start.3
  (19 other events, 43.3 us)
Sparse Core Ops, SparseCore 0:
  539.3 82.4 all-gather.11
  624.0 80.9 all-gather.13
  706.9 85.6 all-gather.15
  794.3 401.9 all-gather.17
  1198.0 210.3 all-gather.19
  1614.2 89.5 reduce-scatter.6
  1706.0 87.9 reduce-scatter.8
  1795.9 226.0 all-gather.21
  2025.6 86.3 reduce-scatter.12
  2115.5 204.7 reduce-scatter.16
  2323.4 221.6 reduce-scatter.10
  2548.1 390.0 reduce-scatter.14
  2941.1 500.9 all-reduce.10
